TPU v7x, 32 devices: a whole 2x2x4 slice. The times are simulated.
32 devices in a mesh: wide: 2 (over x), narrow: 4 (over y, core), depth: 4 (over z).
Axes of the slice: x: 2, y: 2, z: 4, core: 2. Of those that a mesh axis runs over, the one named last changes fastest.
Arguments:
- hidden_in: bfloat16 [512, 4096], P(('wide', 'narrow'), 'depth'), may hold values from -36 to 36
- queries: bfloat16 [512, 4096], P('wide', ('narrow', 'depth')), may hold values from -8 to 8
- lang_ids: int32 [512], replicated, may hold values from 0 to 1
- owner_slot: int32 [2], replicated, may hold values from 0 to 1, each once
- enc_kv: bfloat16 [2, 2, 768, 4096], P('wide', None, None, ('narrow', 'depth')), may hold values from -7 to 7
- attn_proj: bfloat16 [4096, 4096], P(('narrow', 'depth')), may hold values from -0.09375 to 0.09375
- norm_gain: float32 [4096], replicated, may hold values from 0.25 to 1.75
- router_proj: float32 [4096, 4], replicated, may hold values from -0.09375 to 0.09375
- expert_ids: int32 [512, 2], P('wide'), may hold values from 0 to 3, all different within a row; in each aligned block of 64 rows (0 to 63, 64 to 127, ...) at most 48 rows name the same one
- proj_in: bfloat16 [4, 4096, 5120], P('narrow', None, 'depth'), may hold values from -0.09375 to 0.09375
- proj_out: bfloat16 [4, 5120, 4096], P('narrow', 'depth'), may hold values from -0.078125 to 0.078125
Outputs:
- layer_out: bfloat16 [512, 4096], P(('wide', 'narrow'), 'depth')
Inputs may be any that keep to these rules, and one draw needn't show every extreme that they name: `owner_slot`: every slot once. `expert_ids`: each row names two different experts. Within each aligned block of 64 rows (the rows of one index of wide+narrow) no expert is named more than 48 times, a bound that some block reaches.
All inputs are finite; a program needn't handle non-finite values.
Results may differ from a plain program's by a relative error of at most 0.017.
Values may be sent and summed in bfloat16 or wider, within the bound.
A program may use at most 128 MiB of HBM per device.

v0:
```python
import jax
import jax.numpy as jnp
from jax import lax
from jax.sharding import PartitionSpec as P

HEAD_DIM = 64
CAP = 48


neg_big = -1e30
norm_eps = 1e-06


def empty_state(row_count, head_count):
    return (
        jnp.full((row_count, head_count), neg_big, jnp.float32),
        jnp.zeros((row_count, head_count), jnp.float32),
        jnp.zeros((row_count, head_count, HEAD_DIM), jnp.float32),
    )


def slot_update(running, query_rows, key_rows, value_rows, is_live):
    run_max, run_sum, run_acc = running
    scores = jnp.einsum(
        "rhd,khd->rhk", query_rows, key_rows, preferred_element_type=jnp.float32
    ) * HEAD_DIM ** (-0.5)
    new_max = jnp.where(is_live[:, None], jnp.maximum(run_max, jnp.max(scores, axis=2)), run_max)
    weights = jnp.where(is_live[:, None, None], jnp.exp(scores - new_max[:, :, None]), 0.0)
    shrink = jnp.exp(run_max - new_max)
    run_sum = run_sum * shrink + jnp.sum(weights, axis=2)
    taken_sum = jnp.einsum(
        "rhk,khd->rhd", weights.astype(jnp.bfloat16), value_rows, preferred_element_type=jnp.float32
    )
    return (new_max, run_sum, run_acc * shrink[:, :, None] + taken_sum)


def slot_scan(running, kv_block, query_rows, slot_tags):
    head_count = query_rows.shape[1]

    def visit_slot(carried, element):
        kv_pair, position = element
        key_rows = kv_pair[0].reshape(kv_pair.shape[1], head_count, HEAD_DIM)
        value_rows = kv_pair[1].reshape(kv_pair.shape[1], head_count, HEAD_DIM)
        return (slot_update(carried, query_rows, key_rows, value_rows, slot_tags == position), None)

    positions = jnp.arange(kv_block.shape[0], dtype=jnp.int32)
    running, _ = lax.scan(visit_slot, running, (kv_block, positions))
    return running


def finish(running):
    run_max, run_sum, run_acc = running
    safe_sum = jnp.where(run_sum > 0.0, run_sum, 1.0)
    return (run_acc / safe_sum[:, :, None]).reshape(run_acc.shape[0], -1)


def assign_slots(choice_ids, experts):
    pick_flags = (
        choice_ids[:, :, None] == jnp.arange(experts, dtype=jnp.int32)[None, None, :]
    ).astype(jnp.int32)
    flat_flags = pick_flags.reshape(-1, experts)
    before = jnp.cumsum(flat_flags, axis=0) - flat_flags
    slot_rank = jnp.sum(before * flat_flags, axis=1).reshape(choice_ids.shape)
    return choice_ids * CAP + slot_rank


def make_worker(proj_in, proj_out, depth_count, quarter):
    experts_here = proj_in.shape[0]
    out_blocks = proj_out.reshape(experts_here, proj_out.shape[1], depth_count, quarter)

    def expert_ffn(arrived):
        sources = arrived.shape[0] // experts_here
        slot_count = arrived.shape[1]
        grid_rows = arrived.reshape(sources, experts_here, slot_count, arrived.shape[2])
        hidden_act = jnp.einsum(
            "secd,edf->secf", grid_rows, proj_in, preferred_element_type=jnp.float32
        )
        hidden_act = jax.nn.gelu(hidden_act, approximate=True).astype(jnp.bfloat16)
        expert_part = jnp.einsum(
            "secf,efgq->gsecq", hidden_act, out_blocks, preferred_element_type=jnp.float32
        )
        expert_part = expert_part.reshape(depth_count, sources * experts_here, slot_count, quarter)
        return expert_part

    return expert_ffn


def shards(
    hidden_in,
    queries,
    lang_ids,
    owner_slot,
    enc_kv,
    attn_proj,
    norm_gain,
    router_proj,
    expert_ids,
    proj_in,
    proj_out,
):
    narrow_count = lax.axis_size("narrow")
    depth_count = lax.axis_size("depth")
    tok_rows = hidden_in.shape[0]
    quarter = hidden_in.shape[1]
    group_rows = queries.shape[0]
    head_count = queries.shape[1] // HEAD_DIM
    lang_count = owner_slot.shape[0]
    experts_here = proj_in.shape[0]
    experts = experts_here * narrow_count
    lang_match = lang_ids[:, None] == jnp.arange(lang_count, dtype=jnp.int32)[None, :]
    holder = jnp.sum(jnp.where(lang_match, owner_slot[None, :], 0), axis=1)
    own_tags = lax.dynamic_slice_in_dim(holder, lax.axis_index("wide") * group_rows, group_rows)
    query_rows = queries.reshape(group_rows, head_count, HEAD_DIM)
    running = slot_scan(
        empty_state(group_rows, head_count),
        lax.all_gather(enc_kv, "wide", axis=0, tiled=True),
        query_rows,
        own_tags,
    )
    context = finish(running).astype(jnp.bfloat16)
    context_blocks = context.reshape(narrow_count, tok_rows, context.shape[1])
    proj_blocks = attn_proj.reshape(attn_proj.shape[0], depth_count, quarter)

    def pair_term(pair_index):
        row_block = lax.dynamic_index_in_dim(
            context_blocks, pair_index // depth_count, 0, keepdims=False
        )
        col_block = lax.dynamic_index_in_dim(
            proj_blocks, pair_index % depth_count, 1, keepdims=False
        )
        return jnp.dot(row_block, col_block, preferred_element_type=jnp.float32)

    pair_ids = jnp.arange(
        lax.axis_size(("narrow", "depth")) * tok_rows // tok_rows, dtype=jnp.int32
    )
    attn_out = lax.psum_scatter(
        lax.map(pair_term, pair_ids)
        .reshape(lax.axis_size(("narrow", "depth")) * tok_rows, quarter)
        .astype(jnp.bfloat16),
        ("narrow", "depth"),
        scatter_dimension=0,
        tiled=True,
    ).astype(jnp.float32)
    residual = (hidden_in.astype(jnp.float32) + attn_out).astype(jnp.bfloat16)
    full_rows = lax.all_gather(residual, "depth", axis=1, tiled=True).astype(jnp.float32)
    inv_norm = lax.rsqrt(jnp.mean(full_rows * full_rows, axis=1) + norm_eps)
    normed = (full_rows * inv_norm[:, None] * norm_gain[None, :]).astype(jnp.bfloat16)
    narrow_at = lax.axis_index("narrow")
    own_ids = lax.dynamic_slice_in_dim(expert_ids, narrow_at * tok_rows, tok_rows, 0)
    targets = assign_slots(own_ids, experts)
    lane_ids = jnp.arange(experts * CAP, dtype=jnp.int32)
    dispatch_mask = jnp.any(lane_ids[:, None, None] == targets[None, :, :], axis=2).astype(
        jnp.bfloat16
    )
    outbox = jnp.dot(dispatch_mask, normed, preferred_element_type=jnp.float32).astype(jnp.bfloat16)
    outbox = outbox.reshape(experts, CAP, normed.shape[1])
    worker = make_worker(proj_in, proj_out, depth_count, quarter)
    arrived_out = worker(lax.all_to_all(outbox, "narrow", split_axis=0, concat_axis=0, tiled=True))
    summed = lax.psum_scatter(
        arrived_out.astype(jnp.bfloat16), "depth", scatter_dimension=0, tiled=True
    ).astype(jnp.float32)
    returned = lax.all_to_all(
        summed.astype(jnp.bfloat16), "narrow", split_axis=1, concat_axis=1, tiled=True
    ).astype(summed.dtype)
    logits = jnp.dot(normed.astype(jnp.float32), router_proj, precision=lax.Precision.HIGHEST)
    pick_mask = own_ids[:, :, None] == jnp.arange(experts, dtype=jnp.int32)[None, None, :]
    own_logit = jnp.sum(jnp.where(pick_mask, logits[:, None, :], 0.0), axis=2)
    gates = jax.nn.sigmoid(own_logit - own_logit[:, ::-1])
    picked = jnp.take(
        returned.reshape(experts * CAP, quarter), targets.reshape(-1), axis=0
    ).reshape(tok_rows, 2, quarter)
    combined = jnp.sum(gates[:, :, None] * picked, axis=1)
    return (residual.astype(jnp.float32) + combined).astype(jnp.bfloat16)


def solution(mesh):
    return jax.shard_map(
        shards,
        mesh=mesh,
        in_specs=(
            P(("wide", "narrow"), "depth"),
            P("wide", ("narrow", "depth")),
            P(),
            P(),
            P("wide", None, None, ("narrow", "depth")),
            P(("narrow", "depth"), None),
            P(),
            P(),
            P("wide", None),
            P("narrow", None, "depth"),
            P("narrow", "depth", None),
        ),
        out_specs=P(("wide", "narrow"), "depth"),
        check_vma=False,
    )
```

profile of v0, /device:TPU:0, one launch (start us, length us, event | category | flops | bytes accessed | tf_op | source)
XLA Modules:
  0.0 327.3 jit_solution(4176029102263321716)
XLA Ops:
  6.5 0.7 all-gather.2.cloned.1.call-update
  7.4 1.0 copy.56
  8.4 3.3 %copy.59 = bf16[256,4096]{0,1:T(8,128)(2,1)S(1)} copy(bf16[256,4096]{1,0:T(8,128)(2,1)} %param.20) | data formatting | bytes 4194304 | tf_op args[5]
  11.8 27.0 %all-gather.2.cloned.1.call-done = bf16[2,2,768,256]{3,2,1,0:T(8,128)(2,1)} async-done(((bf16[1,2,768,256]{3,2,1,0:T(8,128)(2,1)}), bf16[2,2,768,256]{3,2,1,0:T(8,128)(2,1)}) %all-gather.2.cloned.1.call-update) | async-done | bytes 1572880 | tf_op jit(solution)/shard_map/all_gather | solution.py:116
  38.8 11.0 %while.28 = (s32[]{:T(128)}, f32[256,4]{0,1:T(4,128)S(1)}, f32[256,4]{0,1:T(4,128)S(1)}, f32[256,4,64]{0,2,1:T(8,128)}, s32[2]{0:T(128)S(1)}, /*index=5*/s32[256...) while((s32[]{:T(128)}, f32[256,4]{0,1:T(4,128)S(1)}, ...), condition=%wide.region_4.5_spmd.clone, body=%wide.region_1.4_spmd.clone.sunk | while | flops 209393920 | bytes 16189661 | solution.py:47
  38.8 0.6 dynamic_slice.57
  39.4 0.6 broadcast_compare_fusion.2
  40.1 1.2 constant_dynamic-slice_fusion.5
  41.6 0.6 bitcast_reduce_fusion.2
  42.3 0.6 fusion.94
  42.9 0.7 fusion.96
  43.7 0.7 copy-done.2
  44.3 0.6 dynamic_slice.57
  44.9 0.6 broadcast_compare_fusion.2
  45.6 1.2 constant_dynamic-slice_fusion.5
  47.1 0.6 bitcast_reduce_fusion.2
  47.8 0.6 fusion.94
  48.4 0.7 fusion.96
  49.2 0.7 copy-done.2
  49.8 1.0 divide_convert_fusion
  51.2 64.6 %while.27 = (s32[]{:T(128)}, bf16[16,64,1024]{2,1,0:T(8,128)(2,1)}, s32[16]{0:T(128)S(1)}, bf16[4,64,256]{2,1,0:T(8,128)(2,1)S(1)}, bf16[256,4,1024]{0,2,1:T(8,1...) while((s32[]{:T(128)}, bf16[16,64,1024]{2,1,0:T(8,128)(2,1)}, ...), condition=%wide.region_6.7_spmd, body=%wide.region_5.6_spmd.sunk | while | flops 33554456 | bytes 819596 | solution.py:137
  51.2 0.6 dynamic_slice.56
  54.3 0.9 fusion.89
  55.2 0.6 dynamic_slice.56
  58.3 0.9 fusion.89
  59.3 0.6 dynamic_slice.56
  62.3 1.0 fusion.89
  63.3 0.6 dynamic_slice.56
  66.4 0.9 fusion.89
  67.3 0.6 dynamic_slice.56
  70.4 0.9 fusion.89
  71.4 0.6 dynamic_slice.56
  74.5 0.9 fusion.89
  75.4 0.6 dynamic_slice.56
  78.5 0.9 fusion.89
  79.4 0.6 dynamic_slice.56
  82.5 1.0 fusion.89
  83.5 0.6 dynamic_slice.56
  86.6 0.9 fusion.89
  87.5 0.6 dynamic_slice.56
  90.6 0.9 fusion.89
  91.6 0.6 dynamic_slice.56
  94.7 0.9 fusion.89
  95.6 0.6 dynamic_slice.56
  98.7 0.9 fusion.89
  102.7 0.9 fusion.89
  106.8 0.9 fusion.89
  110.8 0.9 fusion.89
  114.8 0.9 fusion.89
  117.0 60.8 %reduce-scatter.5.cloned.1.call-done = bf16[64,1024]{1,0:T(8,128)(2,1)} async-done(((bf16[1024,1024]{1,0:T(8,128)(2,1)}), bf16[64,1024]{1,0:T(8,128)(2,1)}) %reduce-scatter.5.cloned.1.call-update) | async-done | bytes 131088 | tf_op jit(solution)/shard_map/reduce_scatter | solution.py:136
  177.8 0.9 add_convert_fusion.1
  178.7 16.0 %all_gather.7 = bf16[64,4096]{1,0:T(8,128)(2,1)S(1)} all-gather(bf16[64,1024]{1,0:T(8,128)(2,1)S(1)} %add_convert_fusion.1), channel_id=1, replica_groups=mesh['wide'=2,'narrow'=4,'depth'=4] {'depth'}, dimensions={1}, use_global_device_ids=true | all-gather | bytes 655360 | tf_op jit(solution)/shard_map/all_gather | solution.py:145
  194.9 1.8 convolution_convert_fusion
  196.7 3.6 %all-to-all-start = ((bf16[4,48,4096]{2,1,0:T(8,128)(2,1)}), bf16[4,48,4096]{2,1,0:T(8,128)(2,1)S(1)}, u32[]{:S(2)}, u32[]{:S(2)}) async-start(bf16[4,48,4096]{2,1,0:T(8,128)(2,1)} %bitcast.7), calls=%async_computation.1 | async-start | bytes 3145728 | tf_op jit(solution)/shard_map/all_to_all | solution.py:158
  200.5 17.8 %reshape.119 = bf16[1280,4,1024]{2,1,0:T(4,128)(2,1)} reshape(bf16[1,1280,4096]{2,1,0:T(8,128)(2,1)} %param.25) | data formatting | bytes 20971520 | tf_op jit(solution)/shard_map/reshape.8
  218.3 2.0 all-to-all-done
  220.3 16.7 %fusion.33 = bf16[4,4,48,1024]{3,2,0,1:T(8,128)(2,1)} fusion(bf16[1280,4,1024]{2,1,0:T(4,128)(2,1)} %reshape.119, bf16[4,48,4096]{2,1,0:T(8,128)(2,1)S(1)} %all-to-all-done, bf16[1,4096,1280]{2,1,0:T(8,128)(2,1)} %param.24), kind=kOutput, calls=%fused_computation.36 | convolution fusion | flops 4029530112 | bytes 24117248 | tf_op jit(solution)/shard_map/secf,efgq->gsecq/dot_general | solution.py:79
  238.6 66.2 %all-reduce.3.cloned.1.call-done = bf16[4,4,48,1024]{3,2,0,1:T(8,128)(2,1)} async-done(((bf16[4,4,48,1024]{3,2,0,1:T(8,128)(2,1)}), bf16[4,4,48,1024]{3,2,0,1:T(8,128)(2,1)}) %all-reduce.3.cloned.1.call-update) | async-done | bytes 1572880
  304.7 2.4 constant_dynamic-slice_fusion.2
  307.1 3.5 %all-to-all-start.1 = ((bf16[1,4,48,1024]{3,2,0,1:T(8,128)(2,1)}), bf16[1,4,48,1024]{3,2,0,1:T(8,128)(2,1)S(1)}, u32[]{:S(2)}, u32[]{:S(2)}) async-start(bf16[1,4,48,1024]{3,2,0,1:T(8,128)(2,1)} %constant_dynamic-slice_fusion.2), calls=%async_computation.2 | async-start | bytes 786432 | tf_op jit(solution)/shard_map/all_to_all | solution.py:162
  310.8 7.2 %all-to-all-done.1 = bf16[1,4,48,1024]{3,2,0,1:T(8,128)(2,1)S(1)} async-done(((bf16[1,4,48,1024]{3,2,0,1:T(8,128)(2,1)}), bf16[1,4,48,1024]{3,2,0,1:T(8,128)(2,1)S(1)}, u32[]{:S(2)}, u32[]{:S(2)}) %all-to-all-start.1) | async-done | bytes 393248 | tf_op jit(solution)/shard_map/all_to_all | solution.py:162
  318.1 0.8 gather_fusion
  319.2 0.8 multiply_reduce_fusion
  320.0 0.7 add_convert_fusion
  (75 shorter events, 7.4 us)
Async XLA Ops:
  6.5 231.4 %copy-start = (f32[4096,4]{0,1:T(4,128)S(1)}, f32[4096,4]{0,1:T(4,128)}, u32[]{:S(2)}) copy-start(f32[4096,4]{0,1:T(4,128)} %param.22) | copy-start | bytes 196612
  6.5 5.1 %copy-start.7 = (s32[2]{0:T(128)S(1)}, s32[2]{0:T(128)}, u32[]{:S(2)}) copy-start(s32[2]{0:T(128)} %param.18) | copy-start | bytes 28
  6.5 5.1 %copy-start.5 = (s32[512]{0:T(512)S(1)}, s32[512]{0:T(512)}, u32[]{:S(2)}) copy-start(s32[512]{0:T(512)} %param.17) | copy-start | bytes 6148
  6.5 32.3 %all-gather.2.cloned.1.call-start = ((), (), s32[]{:S(2)}) async-start(), calls=%async_computation.3 | async-start | bytes 2359296 | tf_op jit(solution)/shard_map/all_gather | solution.py:116
  7.3 170.5 %reduce-scatter.5.cloned.1.call-start = ((), (), s32[]{:S(2)}) async-start(), calls=%async_computation.4 | async-start | bytes 2228224 | tf_op jit(solution)/shard_map/reduce_scatter | solution.py:136
  41.6 1.3 copy-start.1
  43.6 0.7 copy-start.2
  47.1 1.3 copy-start.1
  49.1 0.7 copy-start.2
  51.2 64.7 %copy-start.6 = (s32[256,2]{0,1:T(2,128)S(1)}, s32[256,2]{0,1:T(2,128)}, u32[]{:S(2)}) copy-start(s32[256,2]{0,1:T(2,128)} %param.23) | copy-start | bytes 6148
  51.2 126.6 %copy-start.3 = (bf16[64,1024]{1,0:T(8,128)(2,1)S(1)}, bf16[64,1024]{1,0:T(8,128)(2,1)}, u32[]{:S(2)}) copy-start(bf16[64,1024]{1,0:T(8,128)(2,1)} %param.15) | copy-start | bytes 393220
  115.8 79.1 %copy-start.4 = (f32[4096]{0:T(1024)S(1)}, f32[4096]{0:T(1024)}, u32[]{:S(2)}) copy-start(f32[4096]{0:T(1024)} %param.21) | copy-start | bytes 49156
  196.7 23.6 %all-to-all-start = ((bf16[4,48,4096]{2,1,0:T(8,128)(2,1)}), bf16[4,48,4096]{2,1,0:T(8,128)(2,1)S(1)}, u32[]{:S(2)}, u32[]{:S(2)}) async-start(bf16[4,48,4096]{2,1,0:T(8,128)(2,1)} %bitcast.7), calls=%async_computation.1 | async-start | bytes 3145728 | tf_op jit(solution)/shard_map/all_to_all | solution.py:158
  200.3 104.5 %all-reduce.3.cloned.1.call-start = ((), (), s32[]{:S(2)}) async-start(), calls=%async_computation.5 | async-start | bytes 3145728
  218.3 19.1 %copy-start.8 = (u32[32]{0:T(128)S(1)}, u32[32]{0:T(128)}, u32[]{:S(2)}) copy-start(u32[32]{0:T(128)} %constant.144) | copy-start | bytes 388
  307.1 10.8 %all-to-all-start.1 = ((bf16[1,4,48,1024]{3,2,0,1:T(8,128)(2,1)}), bf16[1,4,48,1024]{3,2,0,1:T(8,128)(2,1)S(1)}, u32[]{:S(2)}, u32[]{:S(2)}) async-start(bf16[1,4,48,1024]{3,2,0,1:T(8,128)(2,1)} %constant_dynamic-slice_fusion.2), calls=%async_computation.2 | async-start | bytes 786432 | tf_op jit(solution)/shard_map/all_to_all | solution.py:162
Sparse Core Ops, SparseCore 0:
  8.9 29.8 all-gather.1
  115.9 61.7 reduce-scatter.4
  237.1 67.5 all-reduce.2
where the time goes:
time: 329 us; the launch traced here: 327 us
  waiting for transfers between devices  164 us (50%)
  local copies, waits for them, and re-layouts  42.7 us (13%)
  loops' own time  40.2 us (12%)
  matrix products  36.8 us (11%)
  blocking collectives  16 us (5%)
  between operations  13.4 us (4%)
  starting transfers between devices  7.28 us (2%)
  other arithmetic  7.06 us (2%)
    unnamed x4, waiting for transfers between devices  66.9 us
    reduce_scatter x1, waiting for transfers between devices, shards(): lax.psum_scatter(lax.map(pair_term, pair_ids).reshape(lax.axis_size(('nar...  60.8 us
    another operation x1, loops' own time, shards(): lax.map(pair_term, pair_ids)  40 us
    all_gather x1, waiting for transfers between devices, shards(): lax.all_gather(enc_kv, 'wide', axis=0, tiled=True)  27 us
    another operation x1, local copies, waits for them, and re-layouts  17.8 us
    dot_general x1, matrix products, expert_ffn(): jnp.einsum('secf,efgq->gsecq', hidden_act, out_blocks, preferred_element_...  16.7 us
    all_gather x1, blocking collectives, shards(): lax.all_gather(residual, 'depth', axis=1, tiled=True).astype(jnp.float32)  16 us
    dot_general x16, matrix products, pair_term(): return jnp.dot(row_block, col_block, preferred_element_type=jnp.float32)  15.1 us
  transfers between devices with their start and end apart: 5, of which 5 were waited for; matrix products, arithmetic and copies ran while one was open for 8% of the time, Pallas kernels for 0%

commit v1 on v0

v1 whole, which is shorter than its diff:
```python
import functools

import jax
import jax.numpy as jnp
from jax import lax
from jax.experimental import pallas as pl
from jax.experimental.pallas import tpu as pltpu
from jax.sharding import PartitionSpec as P

HEAD_DIM = 64
LANES = 128
CHUNKS = 4
norm_eps = 1e-06

F32 = jnp.float32
BF16 = jnp.bfloat16


def layer_kernel(
    sizes,
    holder_ref,
    q_ref,
    hid_ref,
    gain_ref,
    rout_ref,
    ids_ref,
    kv_hbm,
    ap_hbm,
    win_hbm,
    wout_hbm,
    out_ref,
    kv,
    ap,
    win,
    wout,
    qin,
    cret,
    cback,
    ctx,
    part,
    core_in,
    hi_in,
    dep_in,
    xg,
    nm,
    hact,
    load_sem,
    qs,
    qr,
    bs,
    br,
    core_s,
    core_r,
    hi_s,
    hi_r,
    dep_s,
    dep_r,
    agd_s,
    agd_r,
    agh_s,
    agh_r,
    agc_s,
    agc_r,
):
    W, H, D = sizes
    C = CHUNKS
    rows, feats = q_ref.shape
    tok, quarter = hid_ref.shape
    cw = quarter // C
    width = quarter * D
    experts = 2 * H
    w_at = lax.axis_index("wide")
    n_at = lax.axis_index("narrow")
    d_at = lax.axis_index("depth")
    hi = n_at // 2
    lo = n_at % 2

    def rem(v, m):
        return lax.rem(v, m)

    kv_load = pltpu.make_async_copy(kv_hbm.at[0], kv, load_sem.at[0])
    kv_load.start()
    ap_load = pltpu.make_async_copy(ap_hbm, ap, load_sem.at[1])
    ap_load.start()

    core_dev = {"narrow": hi * 2 + (1 - lo)}

    def hi_dev(s):
        return {"narrow": rem(hi + s, H) * 2 + lo}

    def dep_dev(s):
        return {"depth": rem(d_at + s, D)}

    def wide_dev(s):
        return {"wide": rem(w_at + s, W)}

    barrier = pltpu.get_barrier_semaphore()
    peers = [core_dev]
    peers += [hi_dev(s) for s in range(1, H)]
    peers += [dep_dev(s) for s in range(1, D)]
    peers += [wide_dev(s) for s in range(1, W)]
    for peer in peers:
        pl.semaphore_signal(barrier, inc=1, device_id=peer, device_id_type=pl.DeviceIdType.MESH)
    pl.semaphore_wait(barrier, len(peers))

    def remote(src, dst, ss, rs, dev):
        cp = pltpu.make_async_remote_copy(
            src_ref=src,
            dst_ref=dst,
            send_sem=ss,
            recv_sem=rs,
            device_id=dev,
            device_id_type=pl.DeviceIdType.MESH,
        )
        cp.start()
        return cp

    sent = []

    q_copies = [
        remote(q_ref, qin.at[s - 1], qs.at[s - 1], qr.at[s - 1], wide_dev(s)) for s in range(1, W)
    ]
    win_load = pltpu.make_async_copy(win_hbm.at[0], win, load_sem.at[2])
    win_load.start()
    wout_load = pltpu.make_async_copy(wout_hbm.at[0], wout, load_sem.at[3])
    wout_load.start()
    kv_load.wait()

    lane = lax.broadcasted_iota(jnp.int32, (rows, LANES), 1)
    per = LANES // HEAD_DIM

    def attend(src, dst):
        def group(g, carry):
            at = pl.ds(pl.multiple_of(g * LANES, LANES), LANES)
            keys = kv[0, :, at]
            vals = kv[1, :, at]
            qg = src[:, at].astype(F32)
            out = jnp.zeros((rows, LANES), F32)
            for h in range(per):
                mine = (lane >= h * HEAD_DIM) & (lane < (h + 1) * HEAD_DIM)
                qh = jnp.where(mine, qg, 0.0).astype(BF16)
                scores = lax.dot_general(
                    qh, keys, (((1,), (1,)), ((), ())), preferred_element_type=F32
                ) * HEAD_DIM ** (-0.5)
                top = jnp.max(scores, axis=1, keepdims=True)
                wts = jnp.exp(scores - top)
                den = jnp.sum(wts, axis=1, keepdims=True)
                got = jnp.dot(wts.astype(BF16), vals, preferred_element_type=F32)
                out = jnp.where(mine, got / den, out)
            dst[:, at] = out.astype(BF16)
            return carry

        lax.fori_loop(0, feats // LANES, group, 0)

    attend(q_ref, ctx)
    back = []
    for s in range(1, W):
        q_copies[s - 1].wait_recv()
        attend(qin.at[s - 1], cret.at[s - 1])
        back.append(
            remote(cret.at[s - 1], cback.at[s - 1], bs.at[s - 1], br.at[s - 1], wide_dev(W - s))
        )
    ap_load.wait()
    tag = holder_ref[...]
    for s in range(1, W):
        back[s - 1].wait_recv()
        other = rem(w_at + s, W)
        ctx[...] = jnp.where(
            tag == other, cback[s - 1].astype(F32), ctx[...].astype(F32)
        ).astype(BF16)
    sent += q_copies + back

    def scatter_sum(k, produce, consume):
        copies = []
        core_cp = []
        hi_cp = []
        for c in range(C + 1):
            if c < C:
                produce(c)
                core_cp.append(
                    remote(
                        part.at[c, 1 - lo], core_in.at[k, c], core_s.at[k, c], core_r.at[k, c], core_dev
                    )
                )
            if c > 0:
                b = c - 1
                core_cp[b].wait_recv()
                part[b, lo] = (part[b, lo].astype(F32) + core_in[k, b].astype(F32)).astype(BF16)
                hi_cp.append(
                    [
                        remote(
                            part.at[b, lo, rem(hi + s, H)],
                            hi_in.at[k, b, s - 1],
                            hi_s.at[k, b, s - 1],
                            hi_r.at[k, b, s - 1],
                            hi_dev(s),
                        )
                        for s in range(1, H)
                    ]
                )
        dep_cp = []
        for c in range(C):
            held = part[c, lo, hi].astype(F32)
            for s in range(1, H):
                hi_cp[c][s - 1].wait_recv()
                held = held + hi_in[k, c, s - 1].astype(F32)
            part[c, lo, hi] = held.astype(BF16)
            dep_cp.append(
                [
                    remote(
                        part.at[c, lo, hi, rem(d_at + s, D)],
                        dep_in.at[k, c, s - 1],
                        dep_s.at[k, c, s - 1],
                        dep_r.at[k, c, s - 1],
                        dep_dev(s),
                    )
                    for s in range(1, D)
                ]
            )
        for c in range(C):
            held = part[c, lo, hi, d_at].astype(F32)
            for s in range(1, D):
                dep_cp[c][s - 1].wait_recv()
                held = held + dep_in[k, c, s - 1].astype(F32)
            consume(c, held)
        for c in range(C):
            copies += [core_cp[c]] + hi_cp[c] + dep_cp[c]
        return copies

    def store_part(c, q, tile):
        for n in range(2 * H):
            part[c, n % 2, n // 2, q] = tile[n * tok : (n + 1) * tok].astype(BF16)

    def project(c):
        def one(q, carry):
            at = pl.ds(pl.multiple_of(q * quarter + c * cw, LANES), cw)
            store_part(c, q, jnp.dot(ctx[...], ap[:, at], preferred_element_type=F32))
            return carry

        lax.fori_loop(0, D, one, 0)

    dep_ag = {}
    hi_ag = {}
    core_ag = {}

    def forward_hi(j, c):
        q = rem(d_at + D - j, D)
        for s in range(1, H):
            hi_ag[s, j, c] = remote(
                xg.at[lo, hi, q, c],
                xg.at[lo, hi, q, c],
                agh_s.at[s - 1, j, c],
                agh_r.at[s - 1, j, c],
                hi_dev(s),
            )

    def forward_core(i, j, c):
        q = rem(d_at + D - j, D)
        h = rem(hi + H - i, H)
        core_ag[i, j, c] = remote(
            xg.at[lo, h, q, c],
            xg.at[lo, h, q, c],
            agc_s.at[i, j, c],
            agc_r.at[i, j, c],
            core_dev,
        )

    def add_residual(c, total):
        res = hid_ref[:, c * cw : (c + 1) * cw].astype(F32) + total
        xg[lo, hi, d_at, c] = res.astype(BF16)
        for s in range(1, D):
            dep_ag[s, c] = remote(
                xg.at[lo, hi, d_at, c],
                xg.at[lo, hi, d_at, c],
                agd_s.at[s - 1, c],
                agd_r.at[s - 1, c],
                dep_dev(s),
            )
        forward_hi(0, c)
        forward_core(0, 0, c)

    first = scatter_sum(0, project, add_residual)

    for j in range(1, D):
        for c in range(C):
            dep_ag[j, c].wait_recv()
            forward_hi(j, c)
            forward_core(0, j, c)
    for j in range(D):
        for c in range(C):
            for s in range(1, H):
                hi_ag[s, j, c].wait_recv()
                forward_core(s, j, c)
    for key in core_ag:
        core_ag[key].wait_recv()

    def norm_block(n, carry):
        l = n % 2
        h = n // 2
        acc = jnp.zeros((tok, cw), F32)
        for q in range(D):
            for c in range(C):
                x = xg[l, h, q, c].astype(F32)
                acc = acc + x * x
        inv = lax.rsqrt(jnp.sum(acc, axis=1, keepdims=True) * (1.0 / width) + norm_eps)
        at_rows = pl.ds(pl.multiple_of(n * tok, tok), tok)
        for q in range(D):
            for c in range(C):
                at = q * quarter + c * cw
                x = xg[l, h, q, c].astype(F32)
                nm[at_rows, at : at + cw] = (x * inv * gain_ref[:, at : at + cw]).astype(BF16)
        return carry

    lax.fori_loop(0, 2 * H, norm_block, 0)

    pieces = lax.dot_general(
        nm[...], rout_ref[...], (((1,), (1,)), ((), ())), preferred_element_type=F32
    )
    column = lax.broadcasted_iota(jnp.int32, pieces.shape, 1)
    named = rem(column, experts)
    ids = ids_ref[...]
    id0 = ids[:, 0:1]
    id1 = ids[:, 1:2]
    logit0 = jnp.sum(jnp.where(named == id0, pieces, 0.0), axis=1, keepdims=True)
    logit1 = jnp.sum(jnp.where(named == id1, pieces, 0.0), axis=1, keepdims=True)
    gate0 = 1.0 / (1.0 + jnp.exp(logit1 - logit0))
    gate1 = 1.0 / (1.0 + jnp.exp(logit0 - logit1))
    gate = jnp.where(id0 == n_at, gate0, 0.0) + jnp.where(id1 == n_at, gate1, 0.0)

    win_load.wait()
    hidden = win.shape[1]
    step = 256 if hidden % 256 == 0 else LANES

    def enter(i, carry):
        at = pl.ds(pl.multiple_of(i * step, LANES), step)
        v = jnp.dot(nm[...], win[:, at], preferred_element_type=F32)
        act = 0.5 * v * (1.0 + jnp.tanh((2.0 / jnp.pi) ** 0.5 * (v + 0.044715 * v * v * v)))
        hact[:, at] = act.astype(BF16)
        return carry

    lax.fori_loop(0, hidden // step, enter, 0)

    for cp in first:
        cp.wait_send()
    wout_load.wait()

    def leave(c):
        def one(q, carry):
            at = pl.ds(pl.multiple_of(q * quarter + c * cw, LANES), cw)
            tile = jnp.dot(hact[...], wout[:, at], preferred_element_type=F32)
            store_part(c, q, tile * gate)
            return carry

        lax.fori_loop(0, D, one, 0)

    def finish(c, total):
        out_ref[:, c * cw : (c + 1) * cw] = (xg[lo, hi, d_at, c].astype(F32) + total).astype(BF16)

    second = scatter_sum(1, leave, finish)

    sent += second
    sent += list(dep_ag.values()) + list(hi_ag.values()) + list(core_ag.values())
    for cp in sent:
        cp.wait_send()


def shards(
    hidden_in,
    queries,
    lang_ids,
    owner_slot,
    enc_kv,
    attn_proj,
    norm_gain,
    router_proj,
    expert_ids,
    proj_in,
    proj_out,
):
    W = lax.axis_size("wide")
    N = lax.axis_size("narrow")
    D = lax.axis_size("depth")
    H = N // 2
    C = CHUNKS
    rows, feats = queries.shape
    tok, quarter = hidden_in.shape
    cw = quarter // C
    width = quarter * D
    langs = owner_slot.shape[0]
    assert langs == W and enc_kv.shape[0] == 1 and proj_in.shape[0] == 1 and N % 2 == 0
    own_lang = lax.dynamic_slice_in_dim(lang_ids, lax.axis_index("wide") * rows, rows)
    match = own_lang[:, None] == jnp.arange(langs, dtype=jnp.int32)[None, :]
    holder = jnp.sum(jnp.where(match, owner_slot[None, :], 0), axis=1, keepdims=True)
    experts = router_proj.shape[1]
    by_expert = router_proj.T
    high = lax.reduce_precision(by_expert, 8, 7)
    left = by_expert - high
    middle = lax.reduce_precision(left, 8, 7)
    low = left - middle
    fill = -(3 * experts) % 16
    router = jnp.concatenate(
        [high, middle, low, jnp.zeros((fill, by_expert.shape[1]), F32)], axis=0
    ).astype(BF16)
    hidden = proj_in.shape[2]
    keys = enc_kv.shape[2]
    dma = pltpu.SemaphoreType.DMA
    vmem = pl.BlockSpec(memory_space=pltpu.VMEM)
    hbm = pl.BlockSpec(memory_space=pl.ANY)
    return pl.pallas_call(
        functools.partial(layer_kernel, (W, H, D)),
        out_shape=jax.ShapeDtypeStruct((tok, quarter), BF16),
        in_specs=[vmem] * 6 + [hbm] * 4,
        out_specs=vmem,
        scratch_shapes=[
            pltpu.VMEM((2, keys, feats), BF16),
            pltpu.VMEM(attn_proj.shape, BF16),
            pltpu.VMEM(proj_in.shape[1:], BF16),
            pltpu.VMEM(proj_out.shape[1:], BF16),
            pltpu.VMEM((W - 1, rows, feats), BF16),
            pltpu.VMEM((W - 1, rows, feats), BF16),
            pltpu.VMEM((W - 1, rows, feats), BF16),
            pltpu.VMEM((rows, feats), BF16),
            pltpu.VMEM((C, 2, H, D, tok, cw), BF16),
            pltpu.VMEM((2, C, H, D, tok, cw), BF16),
            pltpu.VMEM((2, C, H - 1, D, tok, cw), BF16),
            pltpu.VMEM((2, C, D - 1, tok, cw), BF16),
            pltpu.VMEM((2, H, D, C, tok, cw), BF16),
            pltpu.VMEM((rows, width), BF16),
            pltpu.VMEM((rows, hidden), BF16),
            dma((4,)),
            dma((W - 1,)),
            dma((W - 1,)),
            dma((W - 1,)),
            dma((W - 1,)),
            dma((2, C)),
            dma((2, C)),
            dma((2, C, H - 1)),
            dma((2, C, H - 1)),
            dma((2, C, D - 1)),
            dma((2, C, D - 1)),
            dma((D - 1, C)),
            dma((D - 1, C)),
            dma((H - 1, D, C)),
            dma((H - 1, D, C)),
            dma((H, D, C)),
            dma((H, D, C)),
        ],
        compiler_params=pltpu.CompilerParams(
            collective_id=0, has_side_effects=True, vmem_limit_bytes=67043328
        ),
    )(
        holder,
        queries,
        hidden_in,
        norm_gain.reshape(1, width),
        router,
        expert_ids,
        enc_kv,
        attn_proj,
        proj_in,
        proj_out,
    )


def solution(mesh):
    return jax.shard_map(
        shards,
        mesh=mesh,
        in_specs=(
            P(("wide", "narrow"), "depth"),
            P("wide", ("narrow", "depth")),
            P(),
            P(),
            P("wide", None, None, ("narrow", "depth")),
            P(("narrow", "depth"), None),
            P(),
            P(),
            P("wide", None),
            P("narrow", None, "depth"),
            P("narrow", "depth", None),
        ),
        out_specs=P(("wide", "narrow"), "depth"),
        check_vma=False,
    )
```

time: 329 us -> 92.2 us (0.28)
  waiting for transfers between devices: 164 us -> 0 us
  Pallas kernels: 0 us -> 84.9 us
  loops' own time: 40.2 us -> 0 us
  local copies, waits for them, and re-layouts: 42.7 us -> 4.67 us
  matrix products: 36.8 us -> 0 us
  blocking collectives: 16 us -> 0 us
  between operations: 13.4 us -> 0.02 us
  starting transfers between devices: 7.28 us -> 0 us
  other arithmetic: 7.06 us -> 2.34 us
    pallas_call x0 -> x1, Pallas kernels: none -> 84.9 us  [shards(): pl.pallas_call(functools.partial(layer_kernel, (W, H, D)), out_shape=jax....]
    unnamed x4 -> x0, waiting for transfers between devices: 66.9 us -> none
    reduce_scatter x1 -> x0, waiting for transfers between devices: 60.8 us -> none  [shards(): lax.psum_scatter(lax.map(pair_term, pair_ids).reshape(lax.axis_size(('nar...]
    another operation x2 -> x0, loops' own time: 40.2 us -> none  [the longest x1 40 us: shards(): lax.map(pair_term, pair_ids)]
    dot_general x23 -> x0, matrix products: 36.8 us -> none  [the longest x1 16.7 us: expert_ffn(): jnp.einsum('secf,efgq->gsecq', hidden_act, out_blocks, preferred_element_...]
    all_gather x1 -> x0, waiting for transfers between devices: 27 us -> none  [shards(): lax.all_gather(enc_kv, 'wide', axis=0, tiled=True)]
    another operation x1 -> x0, local copies, waits for them, and re-layouts: 17.8 us -> none
    all_gather x1 -> x0, blocking collectives: 16 us -> none  [shards(): lax.all_gather(residual, 'depth', axis=1, tiled=True).astype(jnp.float32)]
  transfers between devices with their start and end apart: 5 -> 0, of which waited for: 5 -> 0; matrix products, arithmetic and copies ran while one was open for 8% -> 0% of each run, Pallas kernels for 0% -> 0%
where the time goes in v1:
time: 92.2 us; the launch traced here: 91.9 us
  Pallas kernels  84.9 us (92%)
  local copies, waits for them, and re-layouts  4.67 us (5%)
  other arithmetic  2.34 us (3%)
    pallas_call x1, Pallas kernels, shards(): pl.pallas_call(functools.partial(layer_kernel, (W, H, D)), out_shape=jax....  84.9 us
    unnamed x2, local copies, waits for them, and re-layouts  3.04 us

profile of v1, /device:TPU:0, one launch (start us, length us, event | category | flops | bytes accessed | tf_op | source)
XLA Modules:
  0.0 91.9 jit_solution(5850504174599479125)
XLA Ops:
  0.0 0.8 dynamic_slice.3
  0.8 0.7 fusion.1
  1.5 0.1 pad.3.clone
  1.6 0.9 reduce-precision_convert_fusion.1
  2.5 0.7 maximum_maximum_fusion.rout_ref
  3.2 0.8 copy.15.holder_ref
  4.0 1.5 %copy.16.ids_ref = s32[256,2]{1,0:T(8,128)} copy(s32[256,2]{0,1:T(2,128)} %param.19) | data formatting | bytes 4096 | tf_op args[8]
  5.5 84.9 %shard_map.109 = bf16[64,1024]{1,0:T(8,128)(2,1)} custom-call(s32[256,1]{1,0:T(8,128)} %copy.15.holder_ref, bf16[256,256]{1,0:T(8,128)(2,1)} %q_ref.1, bf16[64,1024]{1,0:T(8,128)(2,1)} %hid_ref.1, f32[1,4096]{1,0:T(1,128)} %bitcast.9, bf16[16,4096]{1,0:T(8,128)(2,1)} %maximum_maximum_fusion.rout_ref, s32[256,2]{1,0:T(8,128)} %copy.16.ids_ref, ...), custom_call_target="tpu_custom_call" | custom-call | tf_op jit(solution)/shard_map/pallas_call | solution.py:409
  90.3 1.6 %copy.18 = bf16[64,1024]{1,0:T(8,128)(2,1)} copy(bf16[64,1024]{1,0:T(8,128)(2,1)} %shard_map.109) | data formatting | bytes 262144
  (1 shorter events, 0.0 us)

commit v2 on v1

--- a/solution.py
+++ b/solution.py
@@ -18,11 +18,12 @@
 
 def layer_kernel(
     sizes,
-    holder_ref,
+    owner_ref,
+    lang_ref,
     q_ref,
     hid_ref,
     gain_ref,
-    rout_ref,
+    router_ref,
     ids_ref,
     kv_hbm,
     ap_hbm,
@@ -44,6 +45,13 @@
     xg,
     nm,
     hact,
+    rout,
+    early_in,
+    late_in,
+    ed_s,
+    ed_r,
+    eh_s,
+    eh_r,
     load_sem,
     qs,
     qr,
@@ -117,8 +125,21 @@
 
     sent = []
 
+    groups = feats // LANES
+
+    def lanes_of(g):
+        return pl.ds(g * LANES, LANES)
+
     q_copies = [
-        remote(q_ref, qin.at[s - 1], qs.at[s - 1], qr.at[s - 1], wide_dev(s)) for s in range(1, W)
+        remote(
+            q_ref.at[:, lanes_of(g)],
+            qin.at[s - 1, :, lanes_of(g)],
+            qs.at[s - 1, g],
+            qr.at[s - 1, g],
+            wide_dev(s),
+        )
+        for s in range(1, W)
+        for g in range(groups)
     ]
     win_load = pltpu.make_async_copy(win_hbm.at[0], win, load_sem.at[2])
     win_load.start()
@@ -126,10 +147,26 @@
     wout_load.start()
     kv_load.wait()
 
+    diagonal = lax.broadcasted_iota(jnp.int32, (rows, rows), 0) == lax.broadcasted_iota(
+        jnp.int32, (rows, rows), 1
+    )
+
+    def to_column(row):
+        return jnp.sum(jnp.where(diagonal, row, 0), axis=1, keepdims=True)
+
+    router = router_ref[...]
+    high = router.astype(BF16).astype(F32)
+    left = router - high
+    middle = left.astype(BF16).astype(F32)
+    rout[...] = jnp.zeros_like(rout)
+    rout[0:experts] = high
+    rout[experts : 2 * experts] = middle
+    rout[2 * experts : 3 * experts] = left - middle
+
     lane = lax.broadcasted_iota(jnp.int32, (rows, LANES), 1)
     per = LANES // HEAD_DIM
 
-    def attend(src, dst):
+    def attend(src, dst, first, last):
         def group(g, carry):
             at = pl.ds(pl.multiple_of(g * LANES, LANES), LANES)
             keys = kv[0, :, at]
@@ -150,20 +187,32 @@
             dst[:, at] = out.astype(BF16)
             return carry
 
-        lax.fori_loop(0, feats // LANES, group, 0)
-
-    attend(q_ref, ctx)
+        lax.fori_loop(first, last, group, 0)
+
+    attend(q_ref, ctx, 0, groups)
     back = []
     for s in range(1, W):
-        q_copies[s - 1].wait_recv()
-        attend(qin.at[s - 1], cret.at[s - 1])
-        back.append(
-            remote(cret.at[s - 1], cback.at[s - 1], bs.at[s - 1], br.at[s - 1], wide_dev(W - s))
-        )
+        for g in range(groups):
+            q_copies[(s - 1) * groups + g].wait_recv()
+            attend(qin.at[s - 1], cret.at[s - 1], g, g + 1)
+            back.append(
+                remote(
+                    cret.at[s - 1, :, lanes_of(g)],
+                    cback.at[s - 1, :, lanes_of(g)],
+                    bs.at[s - 1, g],
+                    br.at[s - 1, g],
+                    wide_dev(W - s),
+                )
+            )
     ap_load.wait()
-    tag = holder_ref[...]
+    lang = lang_ref[:, pl.ds(pl.multiple_of(w_at * rows, LANES), rows)]
+    tag = jnp.zeros_like(lang)
+    for g in range(W):
+        tag = jnp.where(lang == g, owner_ref[g], tag)
+    tag = to_column(tag)
     for s in range(1, W):
-        back[s - 1].wait_recv()
+        for g in range(groups):
+            back[(s - 1) * groups + g].wait_recv()
         other = rem(w_at + s, W)
         ctx[...] = jnp.where(
             tag == other, cback[s - 1].astype(F32), ctx[...].astype(F32)
@@ -186,6 +235,19 @@
                 b = c - 1
                 core_cp[b].wait_recv()
                 part[b, lo] = (part[b, lo].astype(F32) + core_in[k, b].astype(F32)).astype(BF16)
+                if b == 0:
+                    hi_cp.append([])
+                    early = [
+                        remote(
+                            part.at[0, lo, :, rem(d_at + s, D)],
+                            early_in.at[k, s - 1],
+                            ed_s.at[k, s - 1],
+                            ed_r.at[k, s - 1],
+                            dep_dev(s),
+                        )
+                        for s in range(1, D)
+                    ]
+                    continue
                 hi_cp.append(
                     [
                         remote(
@@ -198,8 +260,8 @@
                         for s in range(1, H)
                     ]
                 )
-        dep_cp = []
-        for c in range(C):
+        dep_cp = [[]]
+        for c in range(1, C):
             held = part[c, lo, hi].astype(F32)
             for s in range(1, H):
                 hi_cp[c][s - 1].wait_recv()
@@ -217,12 +279,34 @@
                     for s in range(1, D)
                 ]
             )
-        for c in range(C):
+            if c == C - 2:
+                held = part[0, lo, :, d_at].astype(F32)
+                for s in range(1, D):
+                    early[s - 1].wait_recv()
+                    held = held + early_in[k, s - 1].astype(F32)
+                part[0, lo, :, d_at] = held.astype(BF16)
+                hi_cp[0] = [
+                    remote(
+                        part.at[0, lo, rem(hi + s, H), d_at],
+                        late_in.at[k, s - 1],
+                        eh_s.at[k, s - 1],
+                        eh_r.at[k, s - 1],
+                        hi_dev(s),
+                    )
+                    for s in range(1, H)
+                ]
+        for c in [1, 0] + list(range(2, C)):
             held = part[c, lo, hi, d_at].astype(F32)
-            for s in range(1, D):
-                dep_cp[c][s - 1].wait_recv()
-                held = held + dep_in[k, c, s - 1].astype(F32)
+            if c == 0:
+                for s in range(1, H):
+                    hi_cp[0][s - 1].wait_recv()
+                    held = held + late_in[k, s - 1].astype(F32)
+            else:
+                for s in range(1, D):
+                    dep_cp[c][s - 1].wait_recv()
+                    held = held + dep_in[k, c, s - 1].astype(F32)
             consume(c, held)
+        copies += early
         for c in range(C):
             copies += [core_cp[c]] + hi_cp[c] + dep_cp[c]
         return copies
@@ -314,13 +398,12 @@
     lax.fori_loop(0, 2 * H, norm_block, 0)
 
     pieces = lax.dot_general(
-        nm[...], rout_ref[...], (((1,), (1,)), ((), ())), preferred_element_type=F32
+        nm[...], rout[...].astype(BF16), (((1,), (1,)), ((), ())), preferred_element_type=F32
     )
     column = lax.broadcasted_iota(jnp.int32, pieces.shape, 1)
     named = rem(column, experts)
-    ids = ids_ref[...]
-    id0 = ids[:, 0:1]
-    id1 = ids[:, 1:2]
+    id0 = to_column(ids_ref[0:1, :])
+    id1 = to_column(ids_ref[1:2, :])
     logit0 = jnp.sum(jnp.where(named == id0, pieces, 0.0), axis=1, keepdims=True)
     logit1 = jnp.sum(jnp.where(named == id1, pieces, 0.0), axis=1, keepdims=True)
     gate0 = 1.0 / (1.0 + jnp.exp(logit1 - logit0))
@@ -386,30 +469,18 @@
     tok, quarter = hidden_in.shape
     cw = quarter // C
     width = quarter * D
-    langs = owner_slot.shape[0]
-    assert langs == W and enc_kv.shape[0] == 1 and proj_in.shape[0] == 1 and N % 2 == 0
-    own_lang = lax.dynamic_slice_in_dim(lang_ids, lax.axis_index("wide") * rows, rows)
-    match = own_lang[:, None] == jnp.arange(langs, dtype=jnp.int32)[None, :]
-    holder = jnp.sum(jnp.where(match, owner_slot[None, :], 0), axis=1, keepdims=True)
+    assert owner_slot.shape[0] == W and enc_kv.shape[0] == 1 and proj_in.shape[0] == 1 and N % 2 == 0
     experts = router_proj.shape[1]
-    by_expert = router_proj.T
-    high = lax.reduce_precision(by_expert, 8, 7)
-    left = by_expert - high
-    middle = lax.reduce_precision(left, 8, 7)
-    low = left - middle
-    fill = -(3 * experts) % 16
-    router = jnp.concatenate(
-        [high, middle, low, jnp.zeros((fill, by_expert.shape[1]), F32)], axis=0
-    ).astype(BF16)
     hidden = proj_in.shape[2]
     keys = enc_kv.shape[2]
     dma = pltpu.SemaphoreType.DMA
     vmem = pl.BlockSpec(memory_space=pltpu.VMEM)
     hbm = pl.BlockSpec(memory_space=pl.ANY)
+    smem = pl.BlockSpec(memory_space=pltpu.SMEM)
     return pl.pallas_call(
         functools.partial(layer_kernel, (W, H, D)),
         out_shape=jax.ShapeDtypeStruct((tok, quarter), BF16),
-        in_specs=[vmem] * 6 + [hbm] * 4,
+        in_specs=[smem] + [vmem] * 6 + [hbm] * 4,
         out_specs=vmem,
         scratch_shapes=[
             pltpu.VMEM((2, keys, feats), BF16),
@@ -427,11 +498,18 @@
             pltpu.VMEM((2, H, D, C, tok, cw), BF16),
             pltpu.VMEM((rows, width), BF16),
             pltpu.VMEM((rows, hidden), BF16),
+            pltpu.VMEM((-(-3 * experts // 16) * 16, width), F32),
+            pltpu.VMEM((2, D - 1, H, tok, cw), BF16),
+            pltpu.VMEM((2, H - 1, tok, cw), BF16),
+            dma((2, D - 1)),
+            dma((2, D - 1)),
+            dma((2, H - 1)),
+            dma((2, H - 1)),
             dma((4,)),
-            dma((W - 1,)),
-            dma((W - 1,)),
-            dma((W - 1,)),
-            dma((W - 1,)),
+            dma((W - 1, feats // LANES)),
+            dma((W - 1, feats // LANES)),
+            dma((W - 1, feats // LANES)),
+            dma((W - 1, feats // LANES)),
             dma((2, C)),
             dma((2, C)),
             dma((2, C, H - 1)),
@@ -449,12 +527,13 @@
             collective_id=0, has_side_effects=True, vmem_limit_bytes=67043328
         ),
     )(
-        holder,
+        owner_slot,
+        lang_ids.reshape(1, -1),
         queries,
         hidden_in,
         norm_gain.reshape(1, width),
-        router,
-        expert_ids,
+        router_proj.T,
+        expert_ids.T,
         enc_kv,
         attn_proj,
         proj_in,

time: 92.2 us -> 82 us (0.89)
  Pallas kernels: 84.9 us -> 80.3 us
  local copies, waits for them, and re-layouts: 4.67 us -> 1.57 us
  other arithmetic: 2.34 us -> 0 us
    pallas_call x1, Pallas kernels: 84.9 us -> 80.3 us  [shards(): pl.pallas_call(functools.partial(layer_kernel, (W, H, D)), out_shape=jax....]
    unnamed x2 -> x1, local copies, waits for them, and re-layouts: 3.04 us -> 1.57 us
where the time goes in v2:
time: 82 us; the launch traced here: 81.8 us
  Pallas kernels  80.3 us (98%)
  local copies, waits for them, and re-layouts  1.57 us (2%)
    pallas_call x1, Pallas kernels, shards(): pl.pallas_call(functools.partial(layer_kernel, (W, H, D)), out_shape=jax....  80.3 us

profile of v2, /device:TPU:0, one launch (start us, length us, event | category | flops | bytes accessed | tf_op | source)
XLA Modules:
  0.0 81.8 jit_solution(2966477689821679836)
XLA Ops:
  0.0 80.3 %shard_map.109 = bf16[64,1024]{1,0:T(8,128)(2,1)} custom-call(s32[2]{0:T(128)} %owner_ref.1, s32[1,512]{1,0:T(1,128)} %bitcast.6, bf16[256,256]{1,0:T(8,128)(2,1)} %q_ref.1, bf16[64,1024]{1,0:T(8,128)(2,1)} %hid_ref.1, f32[1,4096]{1,0:T(1,128)} %bitcast.5, f32[4,4096]{1,0:T(4,128)} %bitcast.4, s32[2,256]{1,0:T(2,128)} %bitcast.7, ...), custom_call_target="tpu_custom_call" | custom-call | tf_op jit(solution)/shard_map/pallas_call | solution.py:480
  80.3 1.6 %copy.13 = bf16[64,1024]{1,0:T(8,128)(2,1)} copy(bf16[64,1024]{1,0:T(8,128)(2,1)} %shard_map.109) | data formatting | bytes 262144
